TPU v7x, 32 devices: a whole 2x2x4 slice. The times are simulated.
32 devices in a mesh: section: 2 (over y), row: 4 (over x, core), col: 4 (over z).
Axes of the slice: x: 2, y: 2, z: 4, core: 2. Of those that a mesh axis runs over, the one named last changes fastest.
Arguments:
- inputs: float32 [3, 128, 16384], P(None, None, ('row', 'col')), may hold values from -512 to 512
- weights: float32 [2, 4, 4, 1024, 16384], P('section', None, 'col', None, 'row'), may hold values from -1 to 1
- norm_gain: float32 [2, 16384], P('section', ('row', 'col')), may hold values from 0.5 to 1.5
Outputs:
- section_outputs: float32 [2, 3, 128, 16384], P('section', None, None, ('row', 'col'))
All inputs are finite; a program needn't handle non-finite values.
Results may differ from a plain program's by a relative error of at most 0.00036.
Values sent between devices are 32-bit elements; how exact they have to be, the bound alone decides.
A program may use at most 192 MiB of HBM per device.

v0:
```python
import jax
import jax.numpy as jnp
from jax import lax
from jax.sharding import PartitionSpec as P


def from_behind(value, axis, steps):
    count = lax.axis_size(axis)
    initial, last = (max(0, -steps), min(count, count - steps))
    return lax.ppermute(value, axis, [(source, source + steps) for source in range(initial, last)])


def split_two(values):
    first = lax.optimization_barrier(values.astype(jnp.bfloat16))
    second = lax.optimization_barrier((values - first.astype(jnp.float32)).astype(jnp.bfloat16))
    return (first, second)


def shards(inputs, weights, norm_gain):
    section_id = lax.axis_index("section")
    row_count = lax.axis_size("row")
    pieces = weights.shape[3]
    out_cols = weights.shape[4]
    flat = weights.reshape(row_count * pieces, out_cols)
    wfirst, wsecond = split_two(flat)
    micro = inputs.shape[0]
    rows = inputs.shape[1]
    gain = norm_gain[0]
    total_features = out_cols * row_count
    received = jnp.zeros((rows, pieces), jnp.float32)
    results = jnp.zeros((micro, rows, pieces), jnp.float32)
    for step in range(micro + 1):
        fresh = inputs[min(step, micro - 1)]
        earlier = inputs[max(step - 1, 0)]
        current = jnp.where(section_id == 0, fresh, earlier + received)
        first, second = split_two(lax.all_gather(current, "row", axis=1, tiled=True))
        double = jnp.concatenate([first, second], axis=0)
        prod_one = jnp.dot(double, wfirst, preferred_element_type=jnp.float32)
        prod_two = jnp.dot(first, wsecond, preferred_element_type=jnp.float32)
        partial_value = prod_one[:rows] + prod_one[rows:] + prod_two
        summed = lax.psum_scatter(partial_value, "col", scatter_dimension=1, tiled=True)
        active = jax.nn.gelu(summed, approximate=True)
        squares = lax.psum(jnp.sum(active * active, axis=1), ("row", "col"))
        scale = lax.rsqrt(squares / total_features + 1e-06)
        normed = active * scale[:, None] * gain[None, :]
        position = step - section_id
        valid = jnp.logical_and(position >= 0, position < micro)
        place = jnp.clip(position, 0, micro - 1)
        former = lax.dynamic_index_in_dim(results, place, 0, keepdims=False)
        results = lax.dynamic_update_index_in_dim(
            results, jnp.where(valid, normed, former), place, 0
        )
        if step < micro:
            received = from_behind(normed, "section", 1)
    return results[None]


def solution(mesh):
    placed = (
        P(None, None, ("row", "col")),
        P("section", None, "col", None, "row"),
        P("section", ("row", "col")),
    )
    return jax.shard_map(
        shards,
        mesh=mesh,
        in_specs=placed,
        out_specs=P("section", None, None, ("row", "col")),
        check_vma=False,
    )
```

profile of v0, /device:TPU:0, one launch (start us, length us, event | category | flops | bytes accessed | tf_op | source)
XLA Modules:
  0.0 658.9 jit_solution(15960127548872160041)
XLA Ops:
  6.5 1.9 slice.38
  8.5 32.8 %bitcast_convert_fusion = bf16[4096,4096]{1,0:T(8,128)(2,1)} fusion(f32[1,4,1,1024,4096]{4,3,2,1,0:T(8,128)} %param.4), kind=kLoop, calls=%fused_computation.1 | loop fusion | flops 16777216 | bytes 100663296 | tf_op jit(solution)/shard_map/convert_element_type | solution.py:14
  41.3 42.3 %fusion = bf16[4096,4096]{1,0:T(8,128)(2,1)} fusion(f32[1,4,1,1024,4096]{4,3,2,1,0:T(8,128)} %param.4, bf16[4096,4096]{1,0:T(8,128)(2,1)} %bitcast_convert_fusion), kind=kLoop, calls=%fused_computation.2 | loop fusion | flops 50331648 | bytes 134217728 | tf_op jit(solution)/shard_map/convert_element_type | solution.py:15
  86.1 15.1 %fusion.2 = f32[256,4096]{1,0:T(8,128)S(1)} fusion(bf16[4096,4096]{1,0:T(8,128)(2,1)} %bitcast_convert_fusion, bf16[128,4096]{1,0:T(8,128)(2,1)S(1)} %fusion.18, bf16[128,4096]{1,0:T(8,128)(2,1)S(1)} %bitcast_convert_fusion.1), kind=kOutput, calls=%fused_computation.12 | convolution fusion | flops 8594128896 | bytes 39845888 | tf_op jit(solution)/shard_map/dot_general | solution.py:38
  101.2 16.6 %fusion.1 = f32[128,4096]{1,0:T(8,128)} fusion(bf16[128,4096]{1,0:T(8,128)(2,1)S(1)} %bitcast_convert_fusion.1, bf16[4096,4096]{1,0:T(8,128)(2,1)} %fusion, f32[256,4096]{1,0:T(8,128)S(1)} %fusion.2), kind=kOutput, calls=%fused_computation.4 | convolution fusion | flops 4296015872 | bytes 40894464 | tf_op jit(solution)/shard_map/dot_general | solution.py:39
  117.9 46.5 %reduce-scatter.5.cloned.1.call-done = f32[128,1024]{1,0:T(8,128)} async-done(((f32[128,4096]{1,0:T(8,128)}), f32[128,1024]{1,0:T(8,128)}) %reduce-scatter.5.cloned.1.call-update) | async-done | bytes 524304 | tf_op jit(solution)/shard_map/reduce_scatter | solution.py:41
  165.7 31.4 %psum.28 = f32[128]{0:T(128)S(1)} all-reduce(f32[128]{0:T(128)S(1)} %multiply_reduce_fusion.3), channel_id=1, replica_groups=mesh['section'=2,'row'=4,'col'=4] {'row','col'}, use_global_device_ids=true, to_apply=%region_2.3 | all-reduce | flops 128 | bytes 1024 | tf_op jit(solution)/shard_map/psum | solution.py:43
  197.4 2.1 bitcast_dynamic-update-slice_fusion.3
  199.4 4.2 collective-permute-start
  203.6 7.8 %collective-permute-done = f32[128,1024]{1,0:T(8,128)} collective-permute-done((f32[128,1024]{1,0:T(8,128)}, f32[128,1024]{1,0:T(8,128)}, u32[]{:S(2)}, u32[]{:S(2)}) %collective-permute-start) | collective-permute-done | bytes 524320 | tf_op jit(solution)/shard_map/ppermute | solution.py:10
  211.4 1.9 fusion.47
  213.6 23.1 %all-gather.6.cloned.1.call-done = f32[128,4096]{1,0:T(8,128)} async-done(((f32[128,1024]{1,0:T(8,128)}), f32[128,4096]{1,0:T(8,128)}) %all-gather.6.cloned.1.call-update) | async-done | bytes 2097168 | tf_op jit(solution)/shard_map/all_gather | solution.py:36
  236.7 1.9 convert_element_type.51
  239.1 16.1 %fusion.6 = f32[256,4096]{1,0:T(8,128)} fusion(bf16[4096,4096]{1,0:T(8,128)(2,1)} %bitcast_convert_fusion, bf16[128,4096]{1,0:T(8,128)(2,1)S(1)} %subtract_convert_fusion.2, bf16[128,4096]{1,0:T(8,128)(2,1)S(1)} %convert_element_type.51), kind=kOutput, calls=%fused_computation.16 | convolution fusion | flops 8594128896 | bytes 39845888 | tf_op jit(solution)/shard_map/dot_general | solution.py:38
  255.2 17.8 %convolution_add_fusion.2 = f32[128,4096]{1,0:T(8,128)} fusion(bf16[128,4096]{1,0:T(8,128)(2,1)S(1)} %convert_element_type.51, bf16[4096,4096]{1,0:T(8,128)(2,1)} %fusion, f32[256,4096]{1,0:T(8,128)} %fusion.6), kind=kOutput, calls=%fused_computation.7 | convolution fusion | flops 4296015872 | bytes 40894464 | tf_op jit(solution)/shard_map/dot_general | solution.py:39
  273.9 42.9 %reduce-scatter.7.cloned.1.call-done = f32[128,1024]{1,0:T(8,128)} async-done(((f32[128,4096]{1,0:T(8,128)}), f32[128,1024]{1,0:T(8,128)}) %reduce-scatter.7.cloned.1.call-update) | async-done | bytes 524304 | tf_op jit(solution)/shard_map/reduce_scatter | solution.py:41
  318.1 31.4 %psum.29 = f32[128]{0:T(128)S(1)} all-reduce(f32[128]{0:T(128)S(1)} %multiply_reduce_fusion.2), channel_id=1, replica_groups=mesh['section'=2,'row'=4,'col'=4] {'row','col'}, use_global_device_ids=true, to_apply=%region_5.6 | all-reduce | flops 128 | bytes 1024 | tf_op jit(solution)/shard_map/psum | solution.py:43
  351.0 3.4 collective-permute-start.1
  354.4 8.3 %collective-permute-done.1 = f32[128,1024]{1,0:T(8,128)S(1)} collective-permute-done((f32[128,1024]{1,0:T(8,128)S(1)}, f32[128,1024]{1,0:T(8,128)S(1)}, u32[]{:S(2)}, u32[]{:S(2)}) %collective-permute-start.1) | collective-permute-done | bytes 524320 | tf_op jit(solution)/shard_map/ppermute | solution.py:10
  363.9 23.0 %all-gather.8.cloned.1.call-done = f32[128,4096]{1,0:T(8,128)} async-done(((f32[128,1024]{1,0:T(8,128)}), f32[128,4096]{1,0:T(8,128)}) %all-gather.8.cloned.1.call-update) | async-done | bytes 2097168 | tf_op jit(solution)/shard_map/all_gather | solution.py:36
  389.3 16.1 %fusion.10 = f32[256,4096]{1,0:T(8,128)} fusion(bf16[4096,4096]{1,0:T(8,128)(2,1)} %bitcast_convert_fusion, bf16[128,4096]{1,0:T(8,128)(2,1)S(1)} %subtract_convert_fusion.1, bf16[128,4096]{1,0:T(8,128)(2,1)S(1)} %convert_element_type.54), kind=kOutput, calls=%fused_computation.20 | convolution fusion | flops 8594128896 | bytes 39845888 | tf_op jit(solution)/shard_map/dot_general | solution.py:38
  405.4 17.8 %convolution_add_fusion.1 = f32[128,4096]{1,0:T(8,128)} fusion(bf16[128,4096]{1,0:T(8,128)(2,1)S(1)} %convert_element_type.54, bf16[4096,4096]{1,0:T(8,128)(2,1)} %fusion, f32[256,4096]{1,0:T(8,128)} %fusion.10), kind=kOutput, calls=%fused_computation.6 | convolution fusion | flops 4296015872 | bytes 40894464 | tf_op jit(solution)/shard_map/dot_general | solution.py:39
  424.1 42.9 %reduce-scatter.9.cloned.1.call-done = f32[128,1024]{1,0:T(8,128)} async-done(((f32[128,4096]{1,0:T(8,128)}), f32[128,1024]{1,0:T(8,128)}) %reduce-scatter.9.cloned.1.call-update) | async-done | bytes 524304 | tf_op jit(solution)/shard_map/reduce_scatter | solution.py:41
  468.4 31.4 %psum.30 = f32[128]{0:T(128)S(1)} all-reduce(f32[128]{0:T(128)S(1)} %multiply_reduce_fusion.1), channel_id=1, replica_groups=mesh['section'=2,'row'=4,'col'=4] {'row','col'}, use_global_device_ids=true, to_apply=%region_8.9 | all-reduce | flops 128 | bytes 1024 | tf_op jit(solution)/shard_map/psum | solution.py:43
  501.2 3.4 collective-permute-start.2
  504.6 8.3 %collective-permute-done.2 = f32[128,1024]{1,0:T(8,128)S(1)} collective-permute-done((f32[128,1024]{1,0:T(8,128)S(1)}, f32[128,1024]{1,0:T(8,128)S(1)}, u32[]{:S(2)}, u32[]{:S(2)}) %collective-permute-start.2) | collective-permute-done | bytes 524320 | tf_op jit(solution)/shard_map/ppermute | solution.py:10
  514.1 23.0 %all-gather.10.cloned.1.call-done = f32[128,4096]{1,0:T(8,128)} async-done(((f32[128,1024]{1,0:T(8,128)}), f32[128,4096]{1,0:T(8,128)}) %all-gather.10.cloned.1.call-update) | async-done | bytes 2097168 | tf_op jit(solution)/shard_map/all_gather | solution.py:36
  539.6 16.1 %fusion.14 = f32[256,4096]{1,0:T(8,128)} fusion(bf16[4096,4096]{1,0:T(8,128)(2,1)} %bitcast_convert_fusion, bf16[128,4096]{1,0:T(8,128)(2,1)S(1)} %subtract_convert_fusion, bf16[128,4096]{1,0:T(8,128)(2,1)S(1)} %convert_element_type.57), kind=kOutput, calls=%fused_computation.24 | convolution fusion | flops 8594128896 | bytes 39845888 | tf_op jit(solution)/shard_map/dot_general | solution.py:38
  555.7 17.8 %convolution_add_fusion = f32[128,4096]{1,0:T(8,128)} fusion(bf16[128,4096]{1,0:T(8,128)(2,1)S(1)} %convert_element_type.57, bf16[4096,4096]{1,0:T(8,128)(2,1)} %fusion, f32[256,4096]{1,0:T(8,128)} %fusion.14), kind=kOutput, calls=%fused_computation.5 | convolution fusion | flops 4296015872 | bytes 40894464 | tf_op jit(solution)/shard_map/dot_general | solution.py:39
  574.6 42.6 %reduce-scatter.11.cloned.1.call-done = f32[128,1024]{1,0:T(8,128)} async-done(((f32[128,4096]{1,0:T(8,128)}), f32[128,1024]{1,0:T(8,128)}) %reduce-scatter.11.cloned.1.call-update) | async-done | bytes 524304 | tf_op jit(solution)/shard_map/reduce_scatter | solution.py:41
  618.6 31.4 %psum.31 = f32[128]{0:T(128)S(1)} all-reduce(f32[128]{0:T(128)S(1)} %multiply_reduce_fusion), channel_id=1, replica_groups=mesh['section'=2,'row'=4,'col'=4] {'row','col'}, use_global_device_ids=true, to_apply=%region_11.12 | all-reduce | flops 128 | bytes 1024 | tf_op jit(solution)/shard_map/psum | solution.py:43
  650.0 2.1 bitcast_dynamic-update-slice_fusion
  (52 shorter events, 21.9 us)
Async XLA Ops:
  6.5 77.1 %all-gather.12.cloned.1.call-start = ((), (), s32[]{:S(2)}) async-start(), calls=%async_computation.11 | async-start | bytes 2621440 | tf_op jit(solution)/shard_map/all_gather | solution.py:36
  8.4 156.0 %reduce-scatter.5.cloned.1.call-start = ((), (), s32[]{:S(2)}) async-start(), calls=%async_computation.4 | async-start | bytes 2621440 | tf_op jit(solution)/shard_map/reduce_scatter | solution.py:41
  83.6 2.2 copy-start
  117.8 79.5 %copy-start.5 = (f32[1,1024]{1,0:T(1,128)S(1)}, f32[1,1024]{1,0:T(1,128)}, u32[]{:S(2)}) copy-start(f32[1,1024]{1,0:T(1,128)} %param.5) | copy-start | bytes 12292
  117.8 93.6 %copy-start.4 = (f32[3,128,1024]{2,1,0:T(8,128)S(1)}, f32[3,128,1024]{2,1,0:T(8,128)}, u32[]{:S(2)}) copy-start(f32[3,128,1024]{2,1,0:T(8,128)} %param.3) | copy-start | bytes 4718596
  117.9 118.8 %all-gather.6.cloned.1.call-start = ((), (), s32[]{:S(2)}) async-start(), calls=%async_computation.5 | async-start | bytes 2621440 | tf_op jit(solution)/shard_map/all_gather | solution.py:36
  199.4 12.0 %collective-permute-start = (f32[128,1024]{1,0:T(8,128)}, f32[128,1024]{1,0:T(8,128)}, u32[]{:S(2)}, u32[]{:S(2)}) collective-permute-start(f32[128,1024]{1,0:T(8,128)} %get-tuple-element.10), channel_id=1, source_target_pairs={{0,16},{1,17},{2,18},{3,19},{4,20},{5,21},{6,22},{7,23},{8,24},{9,... | collective-permute-start | bytes 1572872 | tf_op jit(solution)/shard_map/ppermute | solution.py:10
  213.4 103.4 %reduce-scatter.7.cloned.1.call-start = ((), (), s32[]{:S(2)}) async-start(), calls=%async_computation.6 | async-start | bytes 2621440 | tf_op jit(solution)/shard_map/reduce_scatter | solution.py:41
  236.7 2.2 copy-start.1
  273.0 113.9 %all-gather.8.cloned.1.call-start = ((), (), s32[]{:S(2)}) async-start(), calls=%async_computation.7 | async-start | bytes 2621440 | tf_op jit(solution)/shard_map/all_gather | solution.py:36
  351.0 11.7 %collective-permute-start.1 = (f32[128,1024]{1,0:T(8,128)S(1)}, f32[128,1024]{1,0:T(8,128)S(1)}, u32[]{:S(2)}, u32[]{:S(2)}) collective-permute-start(f32[128,1024]{1,0:T(8,128)S(1)} %get-tuple-element.8), channel_id=1, source_target_pairs={{0,16},{1,17},{2,18},{3,19},{4,20},{5,21},{6,22},{7,23},{8,24},{9,... | collective-permute-start | bytes 1572872 | tf_op jit(solution)/shard_map/ppermute | solution.py:10
  363.6 103.4 %reduce-scatter.9.cloned.1.call-start = ((), (), s32[]{:S(2)}) async-start(), calls=%async_computation.8 | async-start | bytes 2621440 | tf_op jit(solution)/shard_map/reduce_scatter | solution.py:41
  386.9 2.2 copy-start.2
  423.3 113.8 %all-gather.10.cloned.1.call-start = ((), (), s32[]{:S(2)}) async-start(), calls=%async_computation.9 | async-start | bytes 2621440 | tf_op jit(solution)/shard_map/all_gather | solution.py:36
  501.2 11.7 %collective-permute-start.2 = (f32[128,1024]{1,0:T(8,128)S(1)}, f32[128,1024]{1,0:T(8,128)S(1)}, u32[]{:S(2)}, u32[]{:S(2)}) collective-permute-start(f32[128,1024]{1,0:T(8,128)S(1)} %get-tuple-element.6), channel_id=1, source_target_pairs={{0,16},{1,17},{2,18},{3,19},{4,20},{5,21},{6,22},{7,23},{8,24},{9,... | collective-permute-start | bytes 1572872 | tf_op jit(solution)/shard_map/ppermute | solution.py:10
  513.8 103.4 %reduce-scatter.11.cloned.1.call-start = ((), (), s32[]{:S(2)}) async-start(), calls=%async_computation.10 | async-start | bytes 2621440 | tf_op jit(solution)/shard_map/reduce_scatter | solution.py:41
  537.1 2.2 copy-start.3
Sparse Core Ops, SparseCore 0:
  8.9 25.2 all-gather.11
  118.0 46.3 reduce-scatter.4
  213.5 23.1 all-gather.5
  273.2 43.6 reduce-scatter.6
  363.7 23.0 all-gather.7
  423.4 43.6 reduce-scatter.8
  514.0 23.0 all-gather.9
  573.6 43.6 reduce-scatter.10
where the time goes:
time: 660 us; the launch traced here: 659 us
  waiting for transfers between devices  268 us (41%)
  matrix products  133 us (20%)
  blocking collectives  126 us (19%)
  other arithmetic  99.4 us (15%)
  between operations  13.7 us (2%)
  starting transfers between devices  12 us (2%)
    reduce_scatter x4, waiting for transfers between devices, shards(): lax.psum_scatter(partial_value, 'col', scatter_dimension=1, tiled=True)  175 us
    psum x4, blocking collectives, shards(): squares = lax.psum(jnp.sum(active * active, axis=1), ('row', 'col'))  126 us
    dot_general x4, matrix products, shards(): prod_two = jnp.dot(first, wsecond, preferred_element_type=jnp.float32)  70 us
    all_gather x4, waiting for transfers between devices, shards(): lax.all_gather(current, 'row', axis=1, tiled=True)  69 us
    dot_general x4, matrix products, shards(): prod_one = jnp.dot(double, wfirst, preferred_element_type=jnp.float32)  63.4 us
    convert_element_type x5, other arithmetic, split_two(): (values - first.astype(jnp.float32)).astype(jnp.bfloat16)  43.2 us
    convert_element_type x5, other arithmetic, split_two(): first = lax.optimization_barrier(values.astype(jnp.bfloat16))  40.2 us
    ppermute x3, waiting for transfers between devices, from_behind(): lax.ppermute(value, axis, [(source, source + steps) for source in range(i...  24.4 us
  transfers between devices with their start and end apart: 11, of which 10 were waited for; matrix products, arithmetic and copies ran while one was open for 12% of the time, Pallas kernels for 0%

commit v1 on v0

--- a/solution.py
+++ b/solution.py
@@ -2,6 +2,8 @@
 import jax.numpy as jnp
 from jax import lax
 from jax.sharding import PartitionSpec as P
+
+apply_targets_on_mesh = lambda field: lax.psum(lax.psum(field, "row"), "col")
 
 
 def from_behind(value, axis, steps):
@@ -40,7 +42,7 @@
         partial_value = prod_one[:rows] + prod_one[rows:] + prod_two
         summed = lax.psum_scatter(partial_value, "col", scatter_dimension=1, tiled=True)
         active = jax.nn.gelu(summed, approximate=True)
-        squares = lax.psum(jnp.sum(active * active, axis=1), ("row", "col"))
+        squares = apply_targets_on_mesh(jnp.sum(active * active, axis=1))
         scale = lax.rsqrt(squares / total_features + 1e-06)
         normed = active * scale[:, None] * gain[None, :]
         position = step - section_id

time: 660 us -> 596 us (0.903)
  blocking collectives: 126 us -> 65.4 us
    psum x4 -> x8, blocking collectives: 126 us -> 65.4 us  [the longest x4 40.8 us: lax.psum(lax.psum(field, 'row'), 'col')]
  transfers between devices with their start and end apart: 11 -> 11, of which waited for: 10 -> 10; matrix products, arithmetic and copies ran while one was open for 12% -> 13% of each run, Pallas kernels for 0% -> 0%
where the time goes in v1:
time: 596 us; the launch traced here: 595 us
  waiting for transfers between devices  265 us (44%)
  matrix products  134 us (22%)
  other arithmetic  99.4 us (17%)
  blocking collectives  65.4 us (11%)
  between operations  13.7 us (2%)
  starting transfers between devices  12 us (2%)
  local copies, waits for them, and re-layouts  6.28 us (1%)
    reduce_scatter x4, waiting for transfers between devices, shards(): lax.psum_scatter(partial_value, 'col', scatter_dimension=1, tiled=True)  175 us
    dot_general x4, matrix products, shards(): prod_two = jnp.dot(first, wsecond, preferred_element_type=jnp.float32)  70 us
    all_gather x4, waiting for transfers between devices, shards(): lax.all_gather(current, 'row', axis=1, tiled=True)  65.3 us
    dot_general x4, matrix products, shards(): prod_one = jnp.dot(double, wfirst, preferred_element_type=jnp.float32)  63.6 us
    convert_element_type x5, other arithmetic, split_two(): (values - first.astype(jnp.float32)).astype(jnp.bfloat16)  43.3 us
    psum x4, blocking collectives, lax.psum(lax.psum(field, 'row'), 'col')  40.8 us
    convert_element_type x5, other arithmetic, split_two(): first = lax.optimization_barrier(values.astype(jnp.bfloat16))  40.2 us
    ppermute x3, waiting for transfers between devices, from_behind(): lax.ppermute(value, axis, [(source, source + steps) for source in range(i...  24.7 us
  transfers between devices with their start and end apart: 11, of which 10 were waited for; matrix products, arithmetic and copies ran while one was open for 13% of the time, Pallas kernels for 0%

profile of v1, /device:TPU:0, one launch (start us, length us, event | category | flops | bytes accessed | tf_op | source)
XLA Modules:
  0.0 595.4 jit_solution(7304715233619528585)
XLA Ops:
  8.5 32.8 %bitcast_convert_fusion = bf16[4096,4096]{1,0:T(8,128)(2,1)} fusion(f32[1,4,1,1024,4096]{4,3,2,1,0:T(8,128)} %param.4), kind=kLoop, calls=%fused_computation.1 | loop fusion | flops 16777216 | bytes 100663296 | tf_op jit(solution)/shard_map/convert_element_type | solution.py:16
  41.3 42.3 %fusion = bf16[4096,4096]{1,0:T(8,128)(2,1)} fusion(f32[1,4,1,1024,4096]{4,3,2,1,0:T(8,128)} %param.4, bf16[4096,4096]{1,0:T(8,128)(2,1)} %bitcast_convert_fusion), kind=kLoop, calls=%fused_computation.2 | loop fusion | flops 50331648 | bytes 134217728 | tf_op jit(solution)/shard_map/convert_element_type | solution.py:17
  86.1 15.1 %fusion.2 = f32[256,4096]{1,0:T(8,128)S(1)} fusion(bf16[4096,4096]{1,0:T(8,128)(2,1)} %bitcast_convert_fusion, bf16[128,4096]{1,0:T(8,128)(2,1)S(1)} %fusion.18, bf16[128,4096]{1,0:T(8,128)(2,1)S(1)} %bitcast_convert_fusion.1), kind=kOutput, calls=%fused_computation.12 | convolution fusion | flops 8594128896 | bytes 39845888 | tf_op jit(solution)/shard_map/dot_general | solution.py:40
  101.2 16.7 %fusion.1 = f32[128,4096]{1,0:T(8,128)} fusion(bf16[128,4096]{1,0:T(8,128)(2,1)S(1)} %bitcast_convert_fusion.1, bf16[4096,4096]{1,0:T(8,128)(2,1)} %fusion, f32[256,4096]{1,0:T(8,128)S(1)} %fusion.2), kind=kOutput, calls=%fused_computation.4 | convolution fusion | flops 4296015872 | bytes 40894464 | tf_op jit(solution)/shard_map/dot_general | solution.py:41
  118.0 46.5 %reduce-scatter.5.cloned.1.call-done = f32[128,1024]{1,0:T(8,128)} async-done(((f32[128,4096]{1,0:T(8,128)}), f32[128,1024]{1,0:T(8,128)}) %reduce-scatter.5.cloned.1.call-update) | async-done | bytes 524304 | tf_op jit(solution)/shard_map/reduce_scatter | solution.py:43
  165.8 6.1 %psum.56 = f32[128]{0:T(128)S(1)} all-reduce(f32[128]{0:T(128)S(1)} %multiply_reduce_fusion.3), channel_id=1, replica_groups=mesh['section'=2,'row'=4,'col'=4] {'row'}, use_global_device_ids=true, to_apply=%region_2.3 | all-reduce | flops 128 | bytes 1024 | tf_op jit(solution)/shard_map/psum | solution.py:6
  172.0 10.2 %psum.57 = f32[128]{0:T(128)S(1)} all-reduce(f32[128]{0:T(128)S(1)} %psum.56), channel_id=1, replica_groups=mesh['section'=2,'row'=4,'col'=4] {'col'}, use_global_device_ids=true, to_apply=%region_3.4 | all-reduce | flops 128 | bytes 1024 | tf_op jit(solution)/shard_map/psum | solution.py:6
  182.4 2.1 bitcast_dynamic-update-slice_fusion.3
  184.4 4.2 collective-permute-start
  188.6 7.9 %collective-permute-done = f32[128,1024]{1,0:T(8,128)} collective-permute-done((f32[128,1024]{1,0:T(8,128)}, f32[128,1024]{1,0:T(8,128)}, u32[]{:S(2)}, u32[]{:S(2)}) %collective-permute-start) | collective-permute-done | bytes 524320 | tf_op jit(solution)/shard_map/ppermute | solution.py:12
  198.7 21.8 %all-gather.6.cloned.1.call-done = f32[128,4096]{1,0:T(8,128)} async-done(((f32[128,1024]{1,0:T(8,128)}), f32[128,4096]{1,0:T(8,128)}) %all-gather.6.cloned.1.call-update) | async-done | bytes 2097168 | tf_op jit(solution)/shard_map/all_gather | solution.py:38
  223.0 16.1 %fusion.6 = f32[256,4096]{1,0:T(8,128)} fusion(bf16[4096,4096]{1,0:T(8,128)(2,1)} %bitcast_convert_fusion, bf16[128,4096]{1,0:T(8,128)(2,1)S(1)} %subtract_convert_fusion.2, bf16[128,4096]{1,0:T(8,128)(2,1)S(1)} %convert_element_type.51), kind=kOutput, calls=%fused_computation.16 | convolution fusion | flops 8594128896 | bytes 39845888 | tf_op jit(solution)/shard_map/dot_general | solution.py:40
  239.2 17.8 %convolution_add_fusion.2 = f32[128,4096]{1,0:T(8,128)} fusion(bf16[128,4096]{1,0:T(8,128)(2,1)S(1)} %convert_element_type.51, bf16[4096,4096]{1,0:T(8,128)(2,1)} %fusion, f32[256,4096]{1,0:T(8,128)} %fusion.6), kind=kOutput, calls=%fused_computation.7 | convolution fusion | flops 4296015872 | bytes 40894464 | tf_op jit(solution)/shard_map/dot_general | solution.py:41
  257.9 42.9 %reduce-scatter.7.cloned.1.call-done = f32[128,1024]{1,0:T(8,128)} async-done(((f32[128,4096]{1,0:T(8,128)}), f32[128,1024]{1,0:T(8,128)}) %reduce-scatter.7.cloned.1.call-update) | async-done | bytes 524304 | tf_op jit(solution)/shard_map/reduce_scatter | solution.py:43
  302.1 6.1 %psum.58 = f32[128]{0:T(128)S(1)} all-reduce(f32[128]{0:T(128)S(1)} %multiply_reduce_fusion.2), channel_id=1, replica_groups=mesh['section'=2,'row'=4,'col'=4] {'row'}, use_global_device_ids=true, to_apply=%region_6.7 | all-reduce | flops 128 | bytes 1024 | tf_op jit(solution)/shard_map/psum | solution.py:6
  308.2 10.2 %psum.59 = f32[128]{0:T(128)S(1)} all-reduce(f32[128]{0:T(128)S(1)} %psum.58), channel_id=1, replica_groups=mesh['section'=2,'row'=4,'col'=4] {'col'}, use_global_device_ids=true, to_apply=%region_7.8 | all-reduce | flops 128 | bytes 1024 | tf_op jit(solution)/shard_map/psum | solution.py:6
  319.9 3.4 collective-permute-start.1
  323.3 8.4 %collective-permute-done.1 = f32[128,1024]{1,0:T(8,128)S(1)} collective-permute-done((f32[128,1024]{1,0:T(8,128)S(1)}, f32[128,1024]{1,0:T(8,128)S(1)}, u32[]{:S(2)}, u32[]{:S(2)}) %collective-permute-start.1) | collective-permute-done | bytes 524320 | tf_op jit(solution)/shard_map/ppermute | solution.py:12
  332.8 21.8 %all-gather.8.cloned.1.call-done = f32[128,4096]{1,0:T(8,128)} async-done(((f32[128,1024]{1,0:T(8,128)}), f32[128,4096]{1,0:T(8,128)}) %all-gather.8.cloned.1.call-update) | async-done | bytes 2097168 | tf_op jit(solution)/shard_map/all_gather | solution.py:38
  357.1 16.1 %fusion.10 = f32[256,4096]{1,0:T(8,128)} fusion(bf16[4096,4096]{1,0:T(8,128)(2,1)} %bitcast_convert_fusion, bf16[128,4096]{1,0:T(8,128)(2,1)S(1)} %subtract_convert_fusion.1, bf16[128,4096]{1,0:T(8,128)(2,1)S(1)} %convert_element_type.54), kind=kOutput, calls=%fused_computation.20 | convolution fusion | flops 8594128896 | bytes 39845888 | tf_op jit(solution)/shard_map/dot_general | solution.py:40
  373.2 17.8 %convolution_add_fusion.1 = f32[128,4096]{1,0:T(8,128)} fusion(bf16[128,4096]{1,0:T(8,128)(2,1)S(1)} %convert_element_type.54, bf16[4096,4096]{1,0:T(8,128)(2,1)} %fusion, f32[256,4096]{1,0:T(8,128)} %fusion.10), kind=kOutput, calls=%fused_computation.6 | convolution fusion | flops 4296015872 | bytes 40894464 | tf_op jit(solution)/shard_map/dot_general | solution.py:41
  391.9 42.9 %reduce-scatter.9.cloned.1.call-done = f32[128,1024]{1,0:T(8,128)} async-done(((f32[128,4096]{1,0:T(8,128)}), f32[128,1024]{1,0:T(8,128)}) %reduce-scatter.9.cloned.1.call-update) | async-done | bytes 524304 | tf_op jit(solution)/shard_map/reduce_scatter | solution.py:43
  436.1 6.2 %psum.60 = f32[128]{0:T(128)S(1)} all-reduce(f32[128]{0:T(128)S(1)} %multiply_reduce_fusion.1), channel_id=1, replica_groups=mesh['section'=2,'row'=4,'col'=4] {'row'}, use_global_device_ids=true, to_apply=%region_10.11 | all-reduce | flops 128 | bytes 1024 | tf_op jit(solution)/shard_map/psum | solution.py:6
  442.3 10.2 %psum.61 = f32[128]{0:T(128)S(1)} all-reduce(f32[128]{0:T(128)S(1)} %psum.60), channel_id=1, replica_groups=mesh['section'=2,'row'=4,'col'=4] {'col'}, use_global_device_ids=true, to_apply=%region_11.12 | all-reduce | flops 128 | bytes 1024 | tf_op jit(solution)/shard_map/psum | solution.py:6
  453.9 3.4 collective-permute-start.2
  457.3 8.4 %collective-permute-done.2 = f32[128,1024]{1,0:T(8,128)S(1)} collective-permute-done((f32[128,1024]{1,0:T(8,128)S(1)}, f32[128,1024]{1,0:T(8,128)S(1)}, u32[]{:S(2)}, u32[]{:S(2)}) %collective-permute-start.2) | collective-permute-done | bytes 524320 | tf_op jit(solution)/shard_map/ppermute | solution.py:12
  466.9 21.7 %all-gather.10.cloned.1.call-done = f32[128,4096]{1,0:T(8,128)} async-done(((f32[128,1024]{1,0:T(8,128)}), f32[128,4096]{1,0:T(8,128)}) %all-gather.10.cloned.1.call-update) | async-done | bytes 2097168 | tf_op jit(solution)/shard_map/all_gather | solution.py:38
  491.1 16.2 %fusion.14 = f32[256,4096]{1,0:T(8,128)} fusion(bf16[4096,4096]{1,0:T(8,128)(2,1)} %bitcast_convert_fusion, bf16[128,4096]{1,0:T(8,128)(2,1)S(1)} %subtract_convert_fusion, bf16[128,4096]{1,0:T(8,128)(2,1)S(1)} %convert_element_type.57), kind=kOutput, calls=%fused_computation.24 | convolution fusion | flops 8594128896 | bytes 39845888 | tf_op jit(solution)/shard_map/dot_general | solution.py:40
  507.2 17.8 %convolution_add_fusion = f32[128,4096]{1,0:T(8,128)} fusion(bf16[128,4096]{1,0:T(8,128)(2,1)S(1)} %convert_element_type.57, bf16[4096,4096]{1,0:T(8,128)(2,1)} %fusion, f32[256,4096]{1,0:T(8,128)} %fusion.14), kind=kOutput, calls=%fused_computation.5 | convolution fusion | flops 4296015872 | bytes 40894464 | tf_op jit(solution)/shard_map/dot_general | solution.py:41
  526.2 42.6 %reduce-scatter.11.cloned.1.call-done = f32[128,1024]{1,0:T(8,128)} async-done(((f32[128,4096]{1,0:T(8,128)}), f32[128,1024]{1,0:T(8,128)}) %reduce-scatter.11.cloned.1.call-update) | async-done | bytes 524304 | tf_op jit(solution)/shard_map/reduce_scatter | solution.py:43
  570.1 6.2 %psum.62 = f32[128]{0:T(128)S(1)} all-reduce(f32[128]{0:T(128)S(1)} %multiply_reduce_fusion), channel_id=1, replica_groups=mesh['section'=2,'row'=4,'col'=4] {'row'}, use_global_device_ids=true, to_apply=%region_14.15 | all-reduce | flops 128 | bytes 1024 | tf_op jit(solution)/shard_map/psum | solution.py:6
  576.3 10.2 %psum.63 = f32[128]{0:T(128)S(1)} all-reduce(f32[128]{0:T(128)S(1)} %psum.62), channel_id=1, replica_groups=mesh['section'=2,'row'=4,'col'=4] {'col'}, use_global_device_ids=true, to_apply=%region_15.16 | all-reduce | flops 128 | bytes 1024 | tf_op jit(solution)/shard_map/psum | solution.py:6
  (56 shorter events, 29.6 us)
Async XLA Ops:
  6.5 77.1 %all-gather.12.cloned.1.call-start = ((), (), s32[]{:S(2)}) async-start(), calls=%async_computation.11 | async-start | bytes 2621440 | tf_op jit(solution)/shard_map/all_gather | solution.py:38
  8.4 156.1 %reduce-scatter.5.cloned.1.call-start = ((), (), s32[]{:S(2)}) async-start(), calls=%async_computation.4 | async-start | bytes 2621440 | tf_op jit(solution)/shard_map/reduce_scatter | solution.py:43
  83.6 2.2 copy-start
  117.9 64.5 %copy-start.5 = (f32[1,1024]{1,0:T(1,128)S(1)}, f32[1,1024]{1,0:T(1,128)}, u32[]{:S(2)}) copy-start(f32[1,1024]{1,0:T(1,128)} %param.5) | copy-start | bytes 12292
  117.9 78.6 %copy-start.4 = (f32[3,128,1024]{2,1,0:T(8,128)S(1)}, f32[3,128,1024]{2,1,0:T(8,128)}, u32[]{:S(2)}) copy-start(f32[3,128,1024]{2,1,0:T(8,128)} %param.3) | copy-start | bytes 4718596
  118.0 102.6 %all-gather.6.cloned.1.call-start = ((), (), s32[]{:S(2)}) async-start(), calls=%async_computation.5 | async-start | bytes 2621440 | tf_op jit(solution)/shard_map/all_gather | solution.py:38
  184.4 12.1 %collective-permute-start = (f32[128,1024]{1,0:T(8,128)}, f32[128,1024]{1,0:T(8,128)}, u32[]{:S(2)}, u32[]{:S(2)}) collective-permute-start(f32[128,1024]{1,0:T(8,128)} %get-tuple-element.10), channel_id=1, source_target_pairs={{0,16},{1,17},{2,18},{3,19},{4,20},{5,21},{6,22},{7,23},{8,24},{9,... | collective-permute-start | bytes 1572872 | tf_op jit(solution)/shard_map/ppermute | solution.py:12
  198.5 102.3 %reduce-scatter.7.cloned.1.call-start = ((), (), s32[]{:S(2)}) async-start(), calls=%async_computation.6 | async-start | bytes 2621440 | tf_op jit(solution)/shard_map/reduce_scatter | solution.py:43
  220.6 2.2 copy-start.1
  257.0 97.6 %all-gather.8.cloned.1.call-start = ((), (), s32[]{:S(2)}) async-start(), calls=%async_computation.7 | async-start | bytes 2621440 | tf_op jit(solution)/shard_map/all_gather | solution.py:38
  319.9 11.8 %collective-permute-start.1 = (f32[128,1024]{1,0:T(8,128)S(1)}, f32[128,1024]{1,0:T(8,128)S(1)}, u32[]{:S(2)}, u32[]{:S(2)}) collective-permute-start(f32[128,1024]{1,0:T(8,128)S(1)} %get-tuple-element.8), channel_id=1, source_target_pairs={{0,16},{1,17},{2,18},{3,19},{4,20},{5,21},{6,22},{7,23},{8,24},{9,... | collective-permute-start | bytes 1572872 | tf_op jit(solution)/shard_map/ppermute | solution.py:12
  332.6 102.2 %reduce-scatter.9.cloned.1.call-start = ((), (), s32[]{:S(2)}) async-start(), calls=%async_computation.8 | async-start | bytes 2621440 | tf_op jit(solution)/shard_map/reduce_scatter | solution.py:43
  354.6 2.2 copy-start.2
  391.0 97.6 %all-gather.10.cloned.1.call-start = ((), (), s32[]{:S(2)}) async-start(), calls=%async_computation.9 | async-start | bytes 2621440 | tf_op jit(solution)/shard_map/all_gather | solution.py:38
  453.9 11.8 %collective-permute-start.2 = (f32[128,1024]{1,0:T(8,128)S(1)}, f32[128,1024]{1,0:T(8,128)S(1)}, u32[]{:S(2)}, u32[]{:S(2)}) collective-permute-start(f32[128,1024]{1,0:T(8,128)S(1)} %get-tuple-element.6), channel_id=1, source_target_pairs={{0,16},{1,17},{2,18},{3,19},{4,20},{5,21},{6,22},{7,23},{8,24},{9,... | collective-permute-start | bytes 1572872 | tf_op jit(solution)/shard_map/ppermute | solution.py:12
  466.6 102.2 %reduce-scatter.11.cloned.1.call-start = ((), (), s32[]{:S(2)}) async-start(), calls=%async_computation.10 | async-start | bytes 2621440 | tf_op jit(solution)/shard_map/reduce_scatter | solution.py:43
  488.6 2.2 copy-start.3
Sparse Core Ops, SparseCore 0:
  8.9 25.2 all-gather.11
  118.1 46.4 reduce-scatter.4
  198.6 21.8 all-gather.5
  257.1 43.6 reduce-scatter.6
  332.7 21.8 all-gather.7
  391.1 43.6 reduce-scatter.8
  466.7 21.8 all-gather.9
  525.1 43.6 reduce-scatter.10
